TPU v7x, 256 devices: a 2x2x32 block of a 4x8x32 slice. The times are simulated.
256 devices in a mesh: groups: 4 (over y, x), gx: 64 (over z, core).
Axes of the slice: x: 2, y: 2, z: 32, core: 2. Of those that a mesh axis runs over, the one named last changes fastest.
The devices are a block of a 4x8x32 slice.
Arguments:
- tokens: bfloat16 [1536, 4608], P('groups', 'gx'), parts along dimension 0, may hold values from -6 to 6
- gate_weight: bfloat16 [64, 576, 2304], P('gx'), may hold values from -0.09375 to 0.09375
- up_weight: bfloat16 [64, 576, 2304], P('gx'), may hold values from -0.09375 to 0.09375
- down_weight: bfloat16 [64, 2304, 576], P('gx'), may hold values from -0.046875 to 0.046875
Outputs:
- mixed: bfloat16 [1536, 4608], P('groups', 'gx'), parts along dimension 0
There are 4 independent parts, one for each index of `groups`. A program takes and returns all parts, laid end to end along the dimension named above; an argument that names none is the same for every part. Nothing has to cross between parts.
All inputs are finite; a program needn't handle non-finite values.
Results may differ from a plain program's by a relative error of at most 0.015.
Values may be sent and summed in bfloat16 or wider, within the bound.
A program may use at most 128 MiB of HBM per device.

v0:
```python
import jax
import jax.numpy as jnp
from jax import lax
from jax.sharding import PartitionSpec as P

XS = 8


def shifted(block, axis, distance):
    devices = range(lax.axis_size(axis))
    route = [((i - distance) % len(devices), i) for i in devices]
    return lax.ppermute(block, axis, route)


def from_partner(block, axis, bit):
    count = lax.axis_size(axis)
    route = []
    for low in range(count):
        high = low | 1 << bit
        if high != low and high < count:
            route += [(low, high), (high, low)]
    return lax.ppermute(block, axis, route)


def bit_clear(device_index, bit_number):
    return device_index >> bit_number & 1 == 0


def order_pieces(pieces, high_index):
    stacked = jnp.stack(pieces, axis=1)
    rolled = jnp.roll(stacked, high_index, axis=1)
    return rolled.reshape(rolled.shape[0], rolled.shape[1] * rolled.shape[2])


def shards(tokens, gate_weight, up_weight, down_weight):
    gate_tile = gate_weight[0]
    up_tile = up_weight[0]
    down_tile = down_weight[0]
    axis_count = lax.axis_size("gx")
    column_groups = axis_count // XS
    low_bits = XS.bit_length() - 1
    device_index = lax.axis_index("gx")
    high_index = device_index // XS
    received = [tokens]
    for step_count in range(1, column_groups):
        received.append(shifted(tokens, "gx", step_count * XS))
    ordered = [received[0]] + [received[column_groups - j] for j in range(1, column_groups)]
    joined = order_pieces(ordered, high_index)
    gate_part = jnp.dot(joined, gate_tile, preferred_element_type=jnp.float32)
    up_part = jnp.dot(joined, up_tile, preferred_element_type=jnp.float32)
    stacked = jnp.stack([gate_part, up_part])
    for low_step in range(low_bits):
        bit_number = low_bits - 1 - low_step
        half_width = stacked.shape[2] // 2
        lower_half = stacked[:, :, :half_width]
        upper_half = stacked[:, :, half_width:]
        keep_lower = bit_clear(device_index, bit_number)
        outgoing = jnp.where(keep_lower, upper_half, lower_half)
        kept_half = jnp.where(keep_lower, lower_half, upper_half)
        stacked = kept_half + from_partner(outgoing.astype(jnp.bfloat16), "gx", bit_number).astype(
            outgoing.dtype
        )
    hidden = (jax.nn.gelu(stacked[0], approximate=True) * stacked[1]).astype(jnp.bfloat16)
    hidden_received = [hidden]
    for step_count in range(1, column_groups):
        hidden_received.append(shifted(hidden, "gx", step_count * XS))
    hidden_ordered = [hidden_received[0]] + [
        hidden_received[column_groups - j] for j in range(1, column_groups)
    ]
    hidden_joined = order_pieces(hidden_ordered, high_index)
    partial_value = jnp.dot(hidden_joined, down_tile, preferred_element_type=jnp.float32)
    for low_step in range(low_bits):
        bit_number = low_bits - 1 - low_step
        half_width = partial_value.shape[1] // 2
        lower_half = partial_value[:, :half_width]
        upper_half = partial_value[:, half_width:]
        keep_lower = bit_clear(device_index, bit_number)
        outgoing = jnp.where(keep_lower, upper_half, lower_half)
        kept_half = jnp.where(keep_lower, lower_half, upper_half)
        partial_value = kept_half + from_partner(
            outgoing.astype(jnp.bfloat16), "gx", bit_number
        ).astype(outgoing.dtype)
    return partial_value.astype(jnp.bfloat16)


def solution(mesh):
    placed = (P("groups", "gx"), P("gx", None, None), P("gx", None, None), P("gx", None, None))
    return jax.shard_map(
        shards, mesh=mesh, in_specs=placed, out_specs=P("groups", "gx"), check_vma=False
    )
```

profile of v0, /device:TPU:37, one launch (start us, length us, event | category | flops | bytes accessed | tf_op | source)
XLA Modules:
  0.0 402.5 jit_solution(11589440121049348954)
XLA Ops:
  0.0 24.3 %collective-permute-start = (bf16[384,72]{0,1:T(8,128)(2,1)}, bf16[384,72]{0,1:T(8,128)(2,1)}, u32[]{:S(2)}, u32[]{:S(2)}) collective-permute-start(bf16[384,72]{0,1:T(8,128)(2,1)} %param.4), channel_id=1, source_target_pairs={{8,0},{9,1},{10,2},{11,3},{12,4},{13,5},{14,6},{15,7},{16,8},{17,9... | collective-permute-start | bytes 165896 | tf_op jit(solution)/shard_map/ppermute | solution.py:12
  24.3 4.6 %collective-permute-start.1 = (bf16[384,72]{0,1:T(8,128)(2,1)}, bf16[384,72]{0,1:T(8,128)(2,1)}, u32[]{:S(2)}, u32[]{:S(2)}) collective-permute-start(bf16[384,72]{0,1:T(8,128)(2,1)} %param.4), channel_id=1, source_target_pairs={{16,0},{17,1},{18,2},{19,3},{20,4},{21,5},{22,6},{23,7},{24,8},{25... | collective-permute-start | bytes 165896 | tf_op jit(solution)/shard_map/ppermute | solution.py:12
  31.1 15.4 %collective-permute-start.3 = (bf16[384,72]{0,1:T(8,128)(2,1)}, bf16[384,72]{0,1:T(8,128)(2,1)}, u32[]{:S(2)}, u32[]{:S(2)}) collective-permute-start(bf16[384,72]{0,1:T(8,128)(2,1)} %param.4), channel_id=1, source_target_pairs={{32,0},{33,1},{34,2},{35,3},{36,4},{37,5},{38,6},{39,7},{40,8},{41... | collective-permute-start | bytes 165896 | tf_op jit(solution)/shard_map/ppermute | solution.py:12
  47.5 9.6 %collective-permute-start.5 = (bf16[384,72]{0,1:T(8,128)(2,1)}, bf16[384,72]{0,1:T(8,128)(2,1)S(1)}, u32[]{:S(2)}, u32[]{:S(2)}) collective-permute-start(bf16[384,72]{0,1:T(8,128)(2,1)} %param.4), channel_id=1, source_target_pairs={{48,0},{49,1},{50,2},{51,3},{52,4},{53,5},{54,6},{55,7},{56,8},{57... | collective-permute-start | bytes 165896 | tf_op jit(solution)/shard_map/ppermute | solution.py:12
  57.9 5.4 %collective-permute-start.6 = (bf16[384,72]{0,1:T(8,128)(2,1)}, bf16[384,72]{0,1:T(8,128)(2,1)S(1)}, u32[]{:S(2)}, u32[]{:S(2)}) collective-permute-start(bf16[384,72]{0,1:T(8,128)(2,1)} %param.4), channel_id=1, source_target_pairs={{56,0},{57,1},{58,2},{59,3},{60,4},{61,5},{62,6},{63,7},{0,8},{1,9... | collective-permute-start | bytes 165896 | tf_op jit(solution)/shard_map/ppermute | solution.py:12
  66.6 2.9 collective-permute-done.5
  83.3 10.9 %collective-permute-start.7 = (bf16[2,384,1152]{1,2,0:T(8,128)(2,1)}, bf16[2,384,1152]{1,2,0:T(8,128)(2,1)}, u32[]{:S(2)}, u32[]{:S(2)}) collective-permute-start(bf16[2,384,1152]{1,2,0:T(8,128)(2,1)} %select_convert_fusion), channel_id=1, source_target_pairs={{0,4},{4,0},{1,5},{5,1},{2,6},{6,2},{3,7},{7,3},{8,12},{12,8},{9,1... | collective-permute-start | bytes 5308424 | tf_op jit(solution)/shard_map/ppermute | solution.py:22
  94.3 75.2 %collective-permute-done.7 = bf16[2,384,1152]{1,2,0:T(8,128)(2,1)} collective-permute-done((bf16[2,384,1152]{1,2,0:T(8,128)(2,1)}, bf16[2,384,1152]{1,2,0:T(8,128)(2,1)}, u32[]{:S(2)}, u32[]{:S(2)}) %collective-permute-start.7) | collective-permute-done | bytes 1769504 | tf_op jit(solution)/shard_map/ppermute | solution.py:22
  169.5 4.0 convert_add_fusion
  176.4 2.5 collective-permute-start.8
  178.9 18.8 %collective-permute-done.8 = bf16[2,384,576]{1,2,0:T(8,128)(2,1)S(1)} collective-permute-done((bf16[2,384,576]{1,2,0:T(8,128)(2,1)}, bf16[2,384,576]{1,2,0:T(8,128)(2,1)S(1)}, u32[]{:S(2)}, u32[]{:S(2)}) %collective-permute-start.8) | collective-permute-done | bytes 884768 | tf_op jit(solution)/shard_map/ppermute | solution.py:22
  203.9 4.8 %collective-permute-start.10 = (bf16[384,288]{0,1:T(8,128)(2,1)S(1)}, bf16[384,288]{0,1:T(8,128)(2,1)S(1)}, u32[]{:S(2)}, u32[]{:S(2)}) collective-permute-start(bf16[384,288]{0,1:T(8,128)(2,1)S(1)} %fusion.22), channel_id=1, source_target_pairs={{8,0},{9,1},{10,2},{11,3},{12,4},{13,5},{14,6},{15,7},{16,8},{17,9... | collective-permute-start | bytes 663560 | tf_op jit(solution)/shard_map/ppermute | solution.py:12
  208.7 2.5 collective-permute-start.11
  211.2 10.2 %collective-permute-start.12 = (bf16[384,288]{0,1:T(8,128)(2,1)S(1)}, bf16[384,288]{0,1:T(8,128)(2,1)S(1)}, u32[]{:S(2)}, u32[]{:S(2)}) collective-permute-start(bf16[384,288]{0,1:T(8,128)(2,1)S(1)} %fusion.22), channel_id=1, source_target_pairs={{24,0},{25,1},{26,2},{27,3},{28,4},{29,5},{30,6},{31,7},{32,8},{33... | collective-permute-start | bytes 663560 | tf_op jit(solution)/shard_map/ppermute | solution.py:12
  221.4 7.2 %collective-permute-start.13 = (bf16[384,288]{0,1:T(8,128)(2,1)S(1)}, bf16[384,288]{0,1:T(8,128)(2,1)S(1)}, u32[]{:S(2)}, u32[]{:S(2)}) collective-permute-start(bf16[384,288]{0,1:T(8,128)(2,1)S(1)} %fusion.22), channel_id=1, source_target_pairs={{32,0},{33,1},{34,2},{35,3},{36,4},{37,5},{38,6},{39,7},{40,8},{41... | collective-permute-start | bytes 663560 | tf_op jit(solution)/shard_map/ppermute | solution.py:12
  228.6 9.8 %collective-permute-start.14 = (bf16[384,288]{0,1:T(8,128)(2,1)S(1)}, bf16[384,288]{0,1:T(8,128)(2,1)S(1)}, u32[]{:S(2)}, u32[]{:S(2)}) collective-permute-start(bf16[384,288]{0,1:T(8,128)(2,1)S(1)} %fusion.22), channel_id=1, source_target_pairs={{40,0},{41,1},{42,2},{43,3},{44,4},{45,5},{46,6},{47,7},{48,8},{49... | collective-permute-start | bytes 663560 | tf_op jit(solution)/shard_map/ppermute | solution.py:12
  238.6 5.7 %collective-permute-start.15 = (bf16[384,288]{0,1:T(8,128)(2,1)S(1)}, bf16[384,288]{0,1:T(8,128)(2,1)S(1)}, u32[]{:S(2)}, u32[]{:S(2)}) collective-permute-start(bf16[384,288]{0,1:T(8,128)(2,1)S(1)} %fusion.22), channel_id=1, source_target_pairs={{48,0},{49,1},{50,2},{51,3},{52,4},{53,5},{54,6},{55,7},{56,8},{57... | collective-permute-start | bytes 663560 | tf_op jit(solution)/shard_map/ppermute | solution.py:12
  244.3 10.6 %collective-permute-start.16 = (bf16[384,288]{0,1:T(8,128)(2,1)S(1)}, bf16[384,288]{0,1:T(8,128)(2,1)S(1)}, u32[]{:S(2)}, u32[]{:S(2)}) collective-permute-start(bf16[384,288]{0,1:T(8,128)(2,1)S(1)} %fusion.22), channel_id=1, source_target_pairs={{56,0},{57,1},{58,2},{59,3},{60,4},{61,5},{62,6},{63,7},{0,8},{1,9... | collective-permute-start | bytes 663560 | tf_op jit(solution)/shard_map/ppermute | solution.py:12
  254.9 22.3 %collective-permute-done.12 = bf16[384,288]{0,1:T(8,128)(2,1)S(1)} collective-permute-done((bf16[384,288]{0,1:T(8,128)(2,1)S(1)}, bf16[384,288]{0,1:T(8,128)(2,1)S(1)}, u32[]{:S(2)}, u32[]{:S(2)}) %collective-permute-start.12) | collective-permute-done | bytes 221216 | tf_op jit(solution)/shard_map/ppermute | solution.py:12
  277.3 5.5 %collective-permute-done.15 = bf16[384,288]{0,1:T(8,128)(2,1)S(1)} collective-permute-done((bf16[384,288]{0,1:T(8,128)(2,1)S(1)}, bf16[384,288]{0,1:T(8,128)(2,1)S(1)}, u32[]{:S(2)}, u32[]{:S(2)}) %collective-permute-start.15) | collective-permute-done | bytes 221216 | tf_op jit(solution)/shard_map/ppermute | solution.py:12
  282.8 3.7 collective-permute-done.16
  289.9 75.9 %collective-permute-start.17 = (bf16[384,288]{0,1:T(8,128)(2,1)S(1)}, bf16[384,288]{0,1:T(8,128)(2,1)S(1)}, u32[]{:S(2)}, u32[]{:S(2)}) collective-permute-start(bf16[384,288]{0,1:T(8,128)(2,1)S(1)} %select_convert_fusion.3), channel_id=1, source_target_pairs={{0,4},{4,0},{1,5},{5,1},{2,6},{6,2},{3,7},{7,3},{8,12},{12,8},{9,1... | collective-permute-start | bytes 663560 | tf_op jit(solution)/shard_map/ppermute | solution.py:22
  365.8 22.2 %collective-permute-done.17 = bf16[384,288]{0,1:T(8,128)(2,1)S(1)} collective-permute-done((bf16[384,288]{0,1:T(8,128)(2,1)S(1)}, bf16[384,288]{0,1:T(8,128)(2,1)S(1)}, u32[]{:S(2)}, u32[]{:S(2)}) %collective-permute-start.17) | collective-permute-done | bytes 221216 | tf_op jit(solution)/shard_map/ppermute | solution.py:22
  388.1 8.4 %collective-permute-start.18 = (bf16[384,144]{0,1:T(8,128)(2,1)S(1)}, bf16[384,144]{0,1:T(8,128)(2,1)S(1)}, u32[]{:S(2)}, u32[]{:S(2)}) collective-permute-start(bf16[384,144]{0,1:T(8,128)(2,1)S(1)} %select_convert_fusion.4), channel_id=1, source_target_pairs={{0,2},{2,0},{1,3},{3,1},{4,6},{6,4},{5,7},{7,5},{8,10},{10,8},{9,1... | collective-permute-start | bytes 331784 | tf_op jit(solution)/shard_map/ppermute | solution.py:22
  (78 shorter events, 39.6 us)
Async XLA Ops:
  0.0 77.0 %copy-start = (bf16[1,576,2304]{2,1,0:T(8,128)(2,1)S(1)}, bf16[1,576,2304]{2,1,0:T(8,128)(2,1)}, u32[]{:S(2)}) copy-start(bf16[1,576,2304]{2,1,0:T(8,128)(2,1)} %param.6) | copy-start | bytes 7962628
  0.0 47.4 %collective-permute-start = (bf16[384,72]{0,1:T(8,128)(2,1)}, bf16[384,72]{0,1:T(8,128)(2,1)}, u32[]{:S(2)}, u32[]{:S(2)}) collective-permute-start(bf16[384,72]{0,1:T(8,128)(2,1)} %param.4), channel_id=1, source_target_pairs={{8,0},{9,1},{10,2},{11,3},{12,4},{13,5},{14,6},{15,7},{16,8},{17,9... | collective-permute-start | bytes 165896 | tf_op jit(solution)/shard_map/ppermute | solution.py:12
  24.3 33.6 %collective-permute-start.1 = (bf16[384,72]{0,1:T(8,128)(2,1)}, bf16[384,72]{0,1:T(8,128)(2,1)}, u32[]{:S(2)}, u32[]{:S(2)}) collective-permute-start(bf16[384,72]{0,1:T(8,128)(2,1)} %param.4), channel_id=1, source_target_pairs={{16,0},{17,1},{18,2},{19,3},{20,4},{21,5},{22,6},{23,7},{24,8},{25... | collective-permute-start | bytes 165896 | tf_op jit(solution)/shard_map/ppermute | solution.py:12
  28.9 35.2 %collective-permute-start.2 = (bf16[384,72]{0,1:T(8,128)(2,1)}, bf16[384,72]{0,1:T(8,128)(2,1)}, u32[]{:S(2)}, u32[]{:S(2)}) collective-permute-start(bf16[384,72]{0,1:T(8,128)(2,1)} %param.4), channel_id=1, source_target_pairs={{24,0},{25,1},{26,2},{27,3},{28,4},{29,5},{30,6},{31,7},{32,8},{33... | collective-permute-start | bytes 165896 | tf_op jit(solution)/shard_map/ppermute | solution.py:12
  31.1 33.8 %collective-permute-start.3 = (bf16[384,72]{0,1:T(8,128)(2,1)}, bf16[384,72]{0,1:T(8,128)(2,1)}, u32[]{:S(2)}, u32[]{:S(2)}) collective-permute-start(bf16[384,72]{0,1:T(8,128)(2,1)} %param.4), channel_id=1, source_target_pairs={{32,0},{33,1},{34,2},{35,3},{36,4},{37,5},{38,6},{39,7},{40,8},{41... | collective-permute-start | bytes 165896 | tf_op jit(solution)/shard_map/ppermute | solution.py:12
  46.6 19.2 %collective-permute-start.4 = (bf16[384,72]{0,1:T(8,128)(2,1)}, bf16[384,72]{0,1:T(8,128)(2,1)}, u32[]{:S(2)}, u32[]{:S(2)}) collective-permute-start(bf16[384,72]{0,1:T(8,128)(2,1)} %param.4), channel_id=1, source_target_pairs={{40,0},{41,1},{42,2},{43,3},{44,4},{45,5},{46,6},{47,7},{48,8},{49... | collective-permute-start | bytes 165896 | tf_op jit(solution)/shard_map/ppermute | solution.py:12
  47.5 22.1 %collective-permute-start.5 = (bf16[384,72]{0,1:T(8,128)(2,1)}, bf16[384,72]{0,1:T(8,128)(2,1)S(1)}, u32[]{:S(2)}, u32[]{:S(2)}) collective-permute-start(bf16[384,72]{0,1:T(8,128)(2,1)} %param.4), channel_id=1, source_target_pairs={{48,0},{49,1},{50,2},{51,3},{52,4},{53,5},{54,6},{55,7},{56,8},{57... | collective-permute-start | bytes 165896 | tf_op jit(solution)/shard_map/ppermute | solution.py:12
  57.9 14.0 %collective-permute-start.6 = (bf16[384,72]{0,1:T(8,128)(2,1)}, bf16[384,72]{0,1:T(8,128)(2,1)S(1)}, u32[]{:S(2)}, u32[]{:S(2)}) collective-permute-start(bf16[384,72]{0,1:T(8,128)(2,1)} %param.4), channel_id=1, source_target_pairs={{56,0},{57,1},{58,2},{59,3},{60,4},{61,5},{62,6},{63,7},{0,8},{1,9... | collective-permute-start | bytes 165896 | tf_op jit(solution)/shard_map/ppermute | solution.py:12
  77.0 2.0 copy-start.4
  79.0 3.9 copy-start.2
  81.0 2.4 copy-start.3
  83.3 86.2 %collective-permute-start.7 = (bf16[2,384,1152]{1,2,0:T(8,128)(2,1)}, bf16[2,384,1152]{1,2,0:T(8,128)(2,1)}, u32[]{:S(2)}, u32[]{:S(2)}) collective-permute-start(bf16[2,384,1152]{1,2,0:T(8,128)(2,1)} %select_convert_fusion), channel_id=1, source_target_pairs={{0,4},{4,0},{1,5},{5,1},{2,6},{6,2},{3,7},{7,3},{8,12},{12,8},{9,1... | collective-permute-start | bytes 5308424 | tf_op jit(solution)/shard_map/ppermute | solution.py:22
  176.4 21.3 %collective-permute-start.8 = (bf16[2,384,576]{1,2,0:T(8,128)(2,1)}, bf16[2,384,576]{1,2,0:T(8,128)(2,1)S(1)}, u32[]{:S(2)}, u32[]{:S(2)}) collective-permute-start(bf16[2,384,576]{1,2,0:T(8,128)(2,1)} %select_convert_fusion.1), channel_id=1, source_target_pairs={{0,2},{2,0},{1,3},{3,1},{4,6},{6,4},{5,7},{7,5},{8,10},{10,8},{9,1... | collective-permute-start | bytes 2654216 | tf_op jit(solution)/shard_map/ppermute | solution.py:22
  200.0 3.5 collective-permute-start.9
  203.9 34.7 %collective-permute-start.10 = (bf16[384,288]{0,1:T(8,128)(2,1)S(1)}, bf16[384,288]{0,1:T(8,128)(2,1)S(1)}, u32[]{:S(2)}, u32[]{:S(2)}) collective-permute-start(bf16[384,288]{0,1:T(8,128)(2,1)S(1)} %fusion.22), channel_id=1, source_target_pairs={{8,0},{9,1},{10,2},{11,3},{12,4},{13,5},{14,6},{15,7},{16,8},{17,9... | collective-permute-start | bytes 663560 | tf_op jit(solution)/shard_map/ppermute | solution.py:12
  208.7 35.6 %collective-permute-start.11 = (bf16[384,288]{0,1:T(8,128)(2,1)S(1)}, bf16[384,288]{0,1:T(8,128)(2,1)S(1)}, u32[]{:S(2)}, u32[]{:S(2)}) collective-permute-start(bf16[384,288]{0,1:T(8,128)(2,1)S(1)} %fusion.22), channel_id=1, source_target_pairs={{16,0},{17,1},{18,2},{19,3},{20,4},{21,5},{22,6},{23,7},{24,8},{25... | collective-permute-start | bytes 663560 | tf_op jit(solution)/shard_map/ppermute | solution.py:12
  211.2 66.0 %collective-permute-start.12 = (bf16[384,288]{0,1:T(8,128)(2,1)S(1)}, bf16[384,288]{0,1:T(8,128)(2,1)S(1)}, u32[]{:S(2)}, u32[]{:S(2)}) collective-permute-start(bf16[384,288]{0,1:T(8,128)(2,1)S(1)} %fusion.22), channel_id=1, source_target_pairs={{24,0},{25,1},{26,2},{27,3},{28,4},{29,5},{30,6},{31,7},{32,8},{33... | collective-permute-start | bytes 663560 | tf_op jit(solution)/shard_map/ppermute | solution.py:12
  221.4 55.8 %collective-permute-start.13 = (bf16[384,288]{0,1:T(8,128)(2,1)S(1)}, bf16[384,288]{0,1:T(8,128)(2,1)S(1)}, u32[]{:S(2)}, u32[]{:S(2)}) collective-permute-start(bf16[384,288]{0,1:T(8,128)(2,1)S(1)} %fusion.22), channel_id=1, source_target_pairs={{32,0},{33,1},{34,2},{35,3},{36,4},{37,5},{38,6},{39,7},{40,8},{41... | collective-permute-start | bytes 663560 | tf_op jit(solution)/shard_map/ppermute | solution.py:12
  228.6 48.7 %collective-permute-start.14 = (bf16[384,288]{0,1:T(8,128)(2,1)S(1)}, bf16[384,288]{0,1:T(8,128)(2,1)S(1)}, u32[]{:S(2)}, u32[]{:S(2)}) collective-permute-start(bf16[384,288]{0,1:T(8,128)(2,1)S(1)} %fusion.22), channel_id=1, source_target_pairs={{40,0},{41,1},{42,2},{43,3},{44,4},{45,5},{46,6},{47,7},{48,8},{49... | collective-permute-start | bytes 663560 | tf_op jit(solution)/shard_map/ppermute | solution.py:12
  238.6 44.2 %collective-permute-start.15 = (bf16[384,288]{0,1:T(8,128)(2,1)S(1)}, bf16[384,288]{0,1:T(8,128)(2,1)S(1)}, u32[]{:S(2)}, u32[]{:S(2)}) collective-permute-start(bf16[384,288]{0,1:T(8,128)(2,1)S(1)} %fusion.22), channel_id=1, source_target_pairs={{48,0},{49,1},{50,2},{51,3},{52,4},{53,5},{54,6},{55,7},{56,8},{57... | collective-permute-start | bytes 663560 | tf_op jit(solution)/shard_map/ppermute | solution.py:12
  244.3 42.2 %collective-permute-start.16 = (bf16[384,288]{0,1:T(8,128)(2,1)S(1)}, bf16[384,288]{0,1:T(8,128)(2,1)S(1)}, u32[]{:S(2)}, u32[]{:S(2)}) collective-permute-start(bf16[384,288]{0,1:T(8,128)(2,1)S(1)} %fusion.22), channel_id=1, source_target_pairs={{56,0},{57,1},{58,2},{59,3},{60,4},{61,5},{62,6},{63,7},{0,8},{1,9... | collective-permute-start | bytes 663560 | tf_op jit(solution)/shard_map/ppermute | solution.py:12
  289.9 98.1 %collective-permute-start.17 = (bf16[384,288]{0,1:T(8,128)(2,1)S(1)}, bf16[384,288]{0,1:T(8,128)(2,1)S(1)}, u32[]{:S(2)}, u32[]{:S(2)}) collective-permute-start(bf16[384,288]{0,1:T(8,128)(2,1)S(1)} %select_convert_fusion.3), channel_id=1, source_target_pairs={{0,4},{4,0},{1,5},{5,1},{2,6},{6,2},{3,7},{7,3},{8,12},{12,8},{9,1... | collective-permute-start | bytes 663560 | tf_op jit(solution)/shard_map/ppermute | solution.py:22
  388.1 10.5 %collective-permute-start.18 = (bf16[384,144]{0,1:T(8,128)(2,1)S(1)}, bf16[384,144]{0,1:T(8,128)(2,1)S(1)}, u32[]{:S(2)}, u32[]{:S(2)}) collective-permute-start(bf16[384,144]{0,1:T(8,128)(2,1)S(1)} %select_convert_fusion.4), channel_id=1, source_target_pairs={{0,2},{2,0},{1,3},{3,1},{4,6},{6,4},{5,7},{7,5},{8,10},{10,8},{9,1... | collective-permute-start | bytes 331784 | tf_op jit(solution)/shard_map/ppermute | solution.py:22
  398.7 3.1 collective-permute-start.19
  (2 other events, 3.5 us)
where the time goes:
time: 404 us; the launch traced here: 402 us
  starting transfers between devices  214 us (53%)
  waiting for transfers between devices  157 us (39%)
  local copies, waits for them, and re-layouts  14.2 us (4%)
  other arithmetic  10.6 us (3%)
  matrix products  5.4 us (1%)
    ppermute x6, waiting for transfers between devices, from_partner(): return lax.ppermute(block, axis, route)  121 us
    ppermute x14, starting transfers between devices, shifted(): return lax.ppermute(block, axis, route)  112 us
    ppermute x6, starting transfers between devices, from_partner(): return lax.ppermute(block, axis, route)  102 us
    ppermute x14, waiting for transfers between devices, shifted(): return lax.ppermute(block, axis, route)  36.8 us
    unnamed x41, local copies, waits for them, and re-layouts  13.9 us
  transfers between devices with their start and end apart: 20, of which 11 were waited for; matrix products, arithmetic and copies ran while one was open for 1% of the time, Pallas kernels for 0%

commit v1 on v0

v1 whole, which is shorter than its diff:
```python
import functools

import jax
import jax.numpy as jnp
from jax import lax
from jax.experimental import pallas as pl
from jax.experimental.pallas import tpu as pltpu
from jax.sharding import PartitionSpec as P

XS = 8
CORES = 2
Q = XS // CORES
TSPLIT = 3
SSPLIT = 3
MESH = pl.DeviceIdType.MESH


def gelu(v):
    return 0.5 * v * (1.0 + jnp.tanh(0.7978845608 * (v + 0.044715 * v * v * v)))


def kernel(
    G,
    tok_ref,
    gate_hbm,
    up_hbm,
    down_hbm,
    out_ref,
    w_v,
    d_v,
    wt,
    tok,
    x32,
    xb,
    sib_send,
    sib_recv,
    own,
    ch_send,
    ch_recv,
    hbuf,
    acc,
    o_sib_send,
    o_sib_recv,
    o_send,
    o_recv,
    load_sem,
    tok_ss,
    tok_rs,
    sib_ss,
    sib_rs,
    ch_ss,
    ch_rs,
    h_ss,
    h_rs,
    os_ss,
    os_rs,
    o_ss,
    o_rs,
):
    S, T = SSPLIT, TSPLIT
    f = tok_ref.shape[1]
    tokens = tok_ref.shape[0]
    tl = tokens // T
    R = hbuf.shape[2]
    HB = R * S

    me = lax.axis_index("gx")
    a = me // XS
    b = lax.rem(me, XS)
    p = b // CORES
    core = lax.rem(b, CORES)

    step = 1 - 2 * core
    long_n = G // 2
    short_n = G - 1 - long_n
    group_at = lambda k: lax.rem(a + k * step + G, G)
    long_to = group_at(1) * XS + b
    short_to = group_at(-1) * XS + b
    sibling = a * XS + p * CORES + (1 - core)
    chip = lambda q: a * XS + q * CORES + core
    to = lambda index: {"gx": index}

    loads = [
        pltpu.make_async_copy(gate_hbm.at[0], w_v.at[0], load_sem.at[0]),
        pltpu.make_async_copy(up_hbm.at[0], w_v.at[1], load_sem.at[1]),
        pltpu.make_async_copy(down_hbm.at[0], d_v, load_sem.at[2]),
    ]
    for c in loads:
        c.start()

    own_t = tok_ref[...].astype(jnp.float32).T.astype(jnp.bfloat16)
    for t in range(T):
        tok[t, a] = own_t[:, t * tl : (t + 1) * tl]

    barrier = pltpu.get_barrier_semaphore()
    peers = [long_to, short_to, sibling] + [chip(lax.rem(p + j, Q)) for j in range(1, Q)]
    for peer in peers:
        pl.semaphore_signal(barrier, inc=1, device_id=to(peer), device_id_type=MESH)
    pl.semaphore_wait(barrier, len(peers))

    def remote(src, dst, ss, rs, peer):
        return pltpu.make_async_remote_copy(
            src_ref=src, dst_ref=dst, send_sem=ss, recv_sem=rs, device_id=to(peer), device_id_type=MESH
        )

    def ring(buf, ss, rs, i, k, far):
        if far:
            c, peer, e = group_at(-(k - 1)), long_to, k - 1
        else:
            c, peer, e = group_at(k - 1), short_to, long_n + k - 1
        return remote(buf.at[i, c], buf.at[i, c], ss.at[i, e], rs.at[i, e], peer)

    def ring_step(buf, ss, rs, i, k):
        ring(buf, ss, rs, i, k, True).wait_recv()
        if k < long_n:
            ring(buf, ss, rs, i, k + 1, True).start()
        if k <= short_n:
            ring(buf, ss, rs, i, k, False).wait_recv()
            if k < short_n:
                ring(buf, ss, rs, i, k + 1, False).start()

    def ring_start(buf, ss, rs, i):
        ring(buf, ss, rs, i, 1, True).start()
        if short_n:
            ring(buf, ss, rs, i, 1, False).start()

    def ring_drain(buf, ss, rs, i):
        for k in range(1, long_n + 1):
            ring(buf, ss, rs, i, k, True).wait_send()
        for k in range(1, short_n + 1):
            ring(buf, ss, rs, i, k, False).wait_send()

    for t in range(T):
        ring_start(tok, tok_ss, tok_rs, t)

    def turn(g):
        loads[g].wait()
        wide = 128

        def body(j, carry):
            j0 = pl.multiple_of(j * wide, wide)
            wt[g, pl.ds(j0, wide), :] = w_v[g, :, pl.ds(j0, wide)].T
            return carry

        lax.fori_loop(0, w_v.shape[2] // wide, body, 0)

    turn(0)
    for t in range(T):
        ring_step(tok, tok_ss, tok_rs, t, 1)
    turn(1)
    for k in range(2, long_n + 1):
        for t in range(T):
            ring_step(tok, tok_ss, tok_rs, t, k)
    loads[2].wait()

    for t in range(T):
        for c in range(G):
            x32[c * f : (c + 1) * f, t * tl : (t + 1) * tl] = tok[t, c].astype(jnp.float32)
    xb[...] = x32[...].astype(jnp.bfloat16)

    def part(q, g, of_core):
        row = pl.multiple_of((q * CORES + of_core) * HB, 32)
        return jnp.dot(wt[g, pl.ds(row, HB), :], xb[...], preferred_element_type=jnp.float32)

    def sib_part(i, carry):
        q, g = i // 2, lax.rem(i, 2)
        r = part(q, g, 1 - core).astype(jnp.bfloat16)
        for s in range(S):
            sib_send[s, q, g] = r[s * R : (s + 1) * R]
        return carry

    lax.fori_loop(0, Q * 2, sib_part, 0)
    sib = [remote(sib_send.at[s], sib_recv.at[s], sib_ss.at[s], sib_rs.at[s], sibling) for s in range(S)]
    for s in range(S):
        sib[s].start()

    def own_part(i, carry):
        q, g = i // 2, lax.rem(i, 2)
        r = part(q, g, core)
        for s in range(S):
            own[s, q, g] = r[s * R : (s + 1) * R]
        return carry

    lax.fori_loop(0, Q * 2, own_part, 0)

    def chain(d, s, q):
        peer = chip(p + 1) if d == 0 else chip(p - 1)
        return remote(ch_send.at[d, s, q], ch_recv.at[d, s, q], ch_ss.at[d, s, q], ch_rs.at[d, s, q], peer)

    def chain_from(d, s, q):
        peer = chip(p - 1) if d == 0 else chip(p + 1)
        return remote(ch_send.at[d, s, q], ch_recv.at[d, s, q], ch_ss.at[d, s, q], ch_rs.at[d, s, q], peer)

    def is_first(d):
        return p == 0 if d == 0 else p == Q - 1

    def sends(d, q):
        return p < q if d == 0 else p > q

    order = []
    for j in range(Q - 1):
        order += [(0, Q - 1 - j), (1, j)]

    def chain_all(s):
        sib[s].wait_recv()
        for d, q in order:

            @pl.when(jnp.logical_and(is_first(d), sends(d, q)))
            def _():
                ch_send[d, s, q] = (own[s, q] + sib_recv[s, q].astype(jnp.float32)).astype(jnp.bfloat16)
                chain(d, s, q).start()

            @pl.when(jnp.logical_and(jnp.logical_not(is_first(d)), sends(d, q)))
            def _():
                v = own[s, q] + sib_recv[s, q].astype(jnp.float32)
                chain_from(d, s, q).wait_recv()
                ch_send[d, s, q] = (v + ch_recv[d, s, q].astype(jnp.float32)).astype(jnp.bfloat16)
                chain(d, s, q).start()

        own[s, p] = own[s, p] + sib_recv[s, p].astype(jnp.float32)
        for d in range(2):

            @pl.when(jnp.logical_not(is_first(d)))
            def _():
                chain_from(d, s, p).wait_recv()
                own[s, p] = own[s, p] + ch_recv[d, s, p].astype(jnp.float32)

        hbuf[s, a] = (gelu(own[s, p, 0]) * own[s, p, 1]).astype(jnp.bfloat16)
        ring_start(hbuf, h_ss, h_rs, s)

    def chain_drain(s):
        for d, q in order:

            @pl.when(sends(d, q))
            def _():
                chain(d, s, q).wait_send()

    acc[...] = jnp.zeros_like(acc)

    def down(s, c):
        row = pl.multiple_of(c * HB + s * R, 16)
        acc[...] += lax.dot_general(
            d_v[pl.ds(row, R), :], hbuf[s, c], (((0,), (0,)), ((), ())), preferred_element_type=jnp.float32
        )

    def h_step(s, k):
        ring_step(hbuf, h_ss, h_rs, s, k)
        down(s, group_at(-k))
        if k <= short_n:
            down(s, group_at(k))

    for s in range(S):
        chain_all(s)
        down(s, a)
        for j in range(1, s + 1):
            h_step(s - j, j)
    for w in range(S, S + long_n):
        for s in reversed(range(S)):
            if 1 <= w - s <= long_n:
                h_step(s, w - s)

    def block(bb):
        return acc[pl.ds(pl.multiple_of(bb * f, 8), f), :]

    for q in range(Q):
        o_sib_send[q] = block(q * CORES + 1 - core).astype(jnp.bfloat16)
    osib = remote(o_sib_send, o_sib_recv, os_ss, os_rs, sibling)
    osib.start()
    osib.wait_recv()
    outs = []
    for j in range(1, Q):
        q = lax.rem(p + j, Q)
        o_send[j - 1] = (block(q * CORES + core) + o_sib_recv[q].astype(jnp.float32)).astype(jnp.bfloat16)
        c = remote(o_send.at[j - 1], o_recv.at[j - 1], o_ss.at[j - 1], o_rs.at[j - 1], chip(q))
        c.start()
        outs.append(c)
    total = block(b) + o_sib_recv[p].astype(jnp.float32)
    for j, c in enumerate(outs):
        c.wait_recv()
        total = total + o_recv[j].astype(jnp.float32)
    out_ref[...] = total.T.astype(jnp.bfloat16)

    for t in range(T):
        ring_drain(tok, tok_ss, tok_rs, t)
    for s in range(S):
        sib[s].wait_send()
        chain_drain(s)
        ring_drain(hbuf, h_ss, h_rs, s)
    osib.wait_send()
    for c in outs:
        c.wait_send()


def shards(G, tokens, gate_weight, up_weight, down_weight):
    rows, f = tokens.shape
    _, depth, width = gate_weight.shape
    _, down_depth, out_width = down_weight.shape
    hb = width // XS
    R = hb // SSPLIT
    bf, f32 = jnp.bfloat16, jnp.float32
    dma = pltpu.SemaphoreType.DMA
    V = pltpu.VMEM
    return pl.pallas_call(
        functools.partial(kernel, G),
        out_shape=jax.ShapeDtypeStruct((rows, f), bf),
        in_specs=[pl.BlockSpec(memory_space=pltpu.VMEM)] + [pl.BlockSpec(memory_space=pl.ANY)] * 3,
        out_specs=pl.BlockSpec(memory_space=pltpu.VMEM),
        scratch_shapes=[
            V((2, depth, width), bf),
            V((down_depth, out_width), bf),
            V((2, width, depth), bf),
            V((TSPLIT, G, f, rows // TSPLIT), bf),
            V((depth, rows), f32),
            V((depth, rows), bf),
            V((SSPLIT, Q, 2, R, rows), bf),
            V((SSPLIT, Q, 2, R, rows), bf),
            V((SSPLIT, Q, 2, R, rows), f32),
            V((2, SSPLIT, Q, 2, R, rows), bf),
            V((2, SSPLIT, Q, 2, R, rows), bf),
            V((SSPLIT, G, R, rows), bf),
            V((out_width, rows), f32),
            V((Q, f, rows), bf),
            V((Q, f, rows), bf),
            V((Q - 1, f, rows), bf),
            V((Q - 1, f, rows), bf),
            dma((3,)),
            dma((TSPLIT, G - 1)),
            dma((TSPLIT, G - 1)),
            dma((SSPLIT,)),
            dma((SSPLIT,)),
            dma((2, SSPLIT, Q)),
            dma((2, SSPLIT, Q)),
            dma((SSPLIT, G - 1)),
            dma((SSPLIT, G - 1)),
            dma(()),
            dma(()),
            dma((Q - 1,)),
            dma((Q - 1,)),
        ],
        compiler_params=pltpu.CompilerParams(
            collective_id=0, has_side_effects=True, vmem_limit_bytes=60 * 1024 * 1024
        ),
    )(tokens, gate_weight, up_weight, down_weight)


def solution(mesh):
    G = mesh.shape["gx"] // XS
    placed = (P("groups", "gx"), P("gx", None, None), P("gx", None, None), P("gx", None, None))
    return jax.shard_map(
        functools.partial(shards, G), mesh=mesh, in_specs=placed, out_specs=P("groups", "gx"), check_vma=False
    )
```

time: 404 us -> 194 us (0.48)
  starting transfers between devices: 214 us -> 0 us
  Pallas kernels: 0 us -> 186 us
  waiting for transfers between devices: 157 us -> 0 us
  other arithmetic: 10.6 us -> 0 us
  local copies, waits for them, and re-layouts: 14.2 us -> 7.66 us
  matrix products: 5.4 us -> 0 us
    ppermute x20 -> x0, starting transfers between devices: 214 us -> none  [the longest x14 112 us: shifted(): return lax.ppermute(block, axis, route)]
    pallas_call x0 -> x1, Pallas kernels: none -> 186 us  [shards(): pl.pallas_call(functools.partial(kernel, G), out_shape=jax.ShapeDtypeStru...]
    ppermute x20 -> x0, waiting for transfers between devices: 157 us -> none  [the longest x6 121 us: from_partner(): return lax.ppermute(block, axis, route)]
    unnamed x41 -> x2, local copies, waits for them, and re-layouts: 13.9 us -> 6.05 us
    add x5 -> x0, other arithmetic: 6.46 us -> none  [shards(): kept_half + from_partner(outgoing.astype(jnp.bfloat16), 'gx', bit_number)...]
    dot_general x3 -> x0, matrix products: 5.4 us -> none  [the longest x1 1.95 us: shards(): gate_part = jnp.dot(joined, gate_tile, preferred_element_type=jnp.float32)]
  transfers between devices with their start and end apart: 20 -> 0, of which waited for: 11 -> 0; matrix products, arithmetic and copies ran while one was open for 1% -> 0% of each run, Pallas kernels for 0% -> 0%
where the time goes in v1:
time: 194 us
  Pallas kernels  186 us (96%)
  local copies, waits for them, and re-layouts  7.66 us (4%)
    pallas_call x1, Pallas kernels, shards(): pl.pallas_call(functools.partial(kernel, G), out_shape=jax.ShapeDtypeStru...  186 us
    unnamed x2, local copies, waits for them, and re-layouts  6.05 us

profile of v1, /device:TPU:37, one launch (start us, length us, event | category | flops | bytes accessed | tf_op | source)
XLA Modules:
  0.0 194.2 jit_solution(246121232744700485)
XLA Ops:
  0.0 1.6 copy.5.tok_ref
  1.6 4.5 %copy.6.down_hbm = bf16[1,2304,576]{2,1,0:T(8,128)(2,1)} copy(bf16[1,2304,576]{1,2,0:T(8,128)(2,1)} %param.7) | data formatting | bytes 5308416 | tf_op args[3]
  6.1 186.5 %shard_map.46 = bf16[384,72]{1,0:T(8,128)(2,1)} custom-call(bf16[384,72]{1,0:T(8,128)(2,1)} %copy.5.tok_ref, bf16[1,576,2304]{2,1,0:T(8,128)(2,1)} %gate_hbm.1, bf16[1,576,2304]{2,1,0:T(8,128)(2,1)} %up_hbm.1, bf16[1,2304,576]{2,1,0:T(8,128)(2,1)} %copy.6.down_hbm), custom_call_target="tpu_custom_call" | custom-call | tf_op jit(solution)/shard_map/pallas_call | solution.py:303
  192.6 1.6 copy.7

commit v2 on v1

--- a/solution.py
+++ b/solution.py
@@ -1,3 +1,4 @@
+import contextlib
 import functools
 
 import jax
@@ -12,7 +13,13 @@
 Q = XS // CORES
 TSPLIT = 3
 SSPLIT = 3
+HOLD = 5
+PACE = 1.5
 MESH = pl.DeviceIdType.MESH
+
+
+def scope(name):
+    return contextlib.nullcontext()
 
 
 def gelu(v):
@@ -27,6 +34,7 @@
     down_hbm,
     out_ref,
     w_v,
+    dt_v,
     d_v,
     wt,
     tok,
@@ -58,8 +66,7 @@
     o_rs,
 ):
     S, T = SSPLIT, TSPLIT
-    f = tok_ref.shape[1]
-    tokens = tok_ref.shape[0]
+    f, tokens = tok_ref.shape
     tl = tokens // T
     R = hbuf.shape[2]
     HB = R * S
@@ -83,20 +90,20 @@
     loads = [
         pltpu.make_async_copy(gate_hbm.at[0], w_v.at[0], load_sem.at[0]),
         pltpu.make_async_copy(up_hbm.at[0], w_v.at[1], load_sem.at[1]),
-        pltpu.make_async_copy(down_hbm.at[0], d_v, load_sem.at[2]),
+        pltpu.make_async_copy(down_hbm.at[0], dt_v, load_sem.at[2]),
     ]
     for c in loads:
         c.start()
 
-    own_t = tok_ref[...].astype(jnp.float32).T.astype(jnp.bfloat16)
     for t in range(T):
-        tok[t, a] = own_t[:, t * tl : (t + 1) * tl]
+        tok[t, a] = tok_ref[:, t * tl : (t + 1) * tl]
 
     barrier = pltpu.get_barrier_semaphore()
     peers = [long_to, short_to, sibling] + [chip(lax.rem(p + j, Q)) for j in range(1, Q)]
     for peer in peers:
         pl.semaphore_signal(barrier, inc=1, device_id=to(peer), device_id_type=MESH)
-    pl.semaphore_wait(barrier, len(peers))
+    with scope("barrier"):
+        pl.semaphore_wait(barrier, len(peers))
 
     def remote(src, dst, ss, rs, peer):
         return pltpu.make_async_remote_copy(
@@ -133,25 +140,24 @@
     for t in range(T):
         ring_start(tok, tok_ss, tok_rs, t)
 
-    def turn(g):
-        loads[g].wait()
+    def turn(load, src, dst):
+        load.wait()
         wide = 128
 
         def body(j, carry):
             j0 = pl.multiple_of(j * wide, wide)
-            wt[g, pl.ds(j0, wide), :] = w_v[g, :, pl.ds(j0, wide)].T
+            dst[pl.ds(j0, wide), :] = src[:, pl.ds(j0, wide)].T
             return carry
 
-        lax.fori_loop(0, w_v.shape[2] // wide, body, 0)
-
-    turn(0)
-    for t in range(T):
-        ring_step(tok, tok_ss, tok_rs, t, 1)
-    turn(1)
-    for k in range(2, long_n + 1):
+        lax.fori_loop(0, src.shape[1] // wide, body, 0)
+
+    turns = [(loads[0], w_v.at[0], wt.at[0]), (loads[1], w_v.at[1], wt.at[1]), (loads[2], dt_v, d_v)]
+    for k in range(1, long_n + 1):
+        if k <= len(turns):
+            turn(*turns[k - 1])
         for t in range(T):
-            ring_step(tok, tok_ss, tok_rs, t, k)
-    loads[2].wait()
+            with scope(f"tok#k={k}#t={t}"):
+                ring_step(tok, tok_ss, tok_rs, t, k)
 
     for t in range(T):
         for c in range(G):
@@ -169,7 +175,8 @@
             sib_send[s, q, g] = r[s * R : (s + 1) * R]
         return carry
 
-    lax.fori_loop(0, Q * 2, sib_part, 0)
+    with scope("sibpart"):
+        lax.fori_loop(0, Q * 2, sib_part, 0)
     sib = [remote(sib_send.at[s], sib_recv.at[s], sib_ss.at[s], sib_rs.at[s], sibling) for s in range(S)]
     for s in range(S):
         sib[s].start()
@@ -181,7 +188,8 @@
             own[s, q, g] = r[s * R : (s + 1) * R]
         return carry
 
-    lax.fori_loop(0, Q * 2, own_part, 0)
+    with scope("ownpart"):
+        lax.fori_loop(0, Q * 2, own_part, 0)
 
     def chain(d, s, q):
         peer = chip(p + 1) if d == 0 else chip(p - 1)
@@ -197,26 +205,20 @@
     def sends(d, q):
         return p < q if d == 0 else p > q
 
-    order = []
-    for j in range(Q - 1):
-        order += [(0, Q - 1 - j), (1, j)]
-
-    def chain_all(s):
-        sib[s].wait_recv()
-        for d, q in order:
-
-            @pl.when(jnp.logical_and(is_first(d), sends(d, q)))
+    def chain_step(s, depth):
+        for d in range(2):
+
+            @pl.when(p == (depth if d == 0 else Q - 1 - depth))
             def _():
-                ch_send[d, s, q] = (own[s, q] + sib_recv[s, q].astype(jnp.float32)).astype(jnp.bfloat16)
-                chain(d, s, q).start()
-
-            @pl.when(jnp.logical_and(jnp.logical_not(is_first(d)), sends(d, q)))
-            def _():
-                v = own[s, q] + sib_recv[s, q].astype(jnp.float32)
-                chain_from(d, s, q).wait_recv()
-                ch_send[d, s, q] = (v + ch_recv[d, s, q].astype(jnp.float32)).astype(jnp.bfloat16)
-                chain(d, s, q).start()
-
+                for q in range(Q - 1, depth, -1) if d == 0 else range(Q - 1 - depth):
+                    v = own[s, q] + sib_recv[s, q].astype(jnp.float32)
+                    if depth > 0:
+                        chain_from(d, s, q).wait_recv()
+                        v = v + ch_recv[d, s, q].astype(jnp.float32)
+                    ch_send[d, s, q] = v.astype(jnp.bfloat16)
+                    chain(d, s, q).start()
+
+    def finish(s):
         own[s, p] = own[s, p] + sib_recv[s, p].astype(jnp.float32)
         for d in range(2):
 
@@ -227,13 +229,15 @@
 
         hbuf[s, a] = (gelu(own[s, p, 0]) * own[s, p, 1]).astype(jnp.bfloat16)
         ring_start(hbuf, h_ss, h_rs, s)
+        down(s, a)
 
     def chain_drain(s):
-        for d, q in order:
-
-            @pl.when(sends(d, q))
-            def _():
-                chain(d, s, q).wait_send()
+        for d in range(2):
+            for q in range(Q):
+
+                @pl.when(sends(d, q))
+                def _():
+                    chain(d, s, q).wait_send()
 
     acc[...] = jnp.zeros_like(acc)
 
@@ -244,20 +248,35 @@
         )
 
     def h_step(s, k):
-        ring_step(hbuf, h_ss, h_rs, s, k)
+        with scope(f"hwait#s={s}#k={k}"):
+            ring_step(hbuf, h_ss, h_rs, s, k)
         down(s, group_at(-k))
         if k <= short_n:
             down(s, group_at(k))
 
+    inner = jnp.logical_and(p > 0, p < Q - 1)
+    events = []
     for s in range(S):
-        chain_all(s)
-        down(s, a)
-        for j in range(1, s + 1):
-            h_step(s - j, j)
-    for w in range(S, S + long_n):
-        for s in reversed(range(S)):
-            if 1 <= w - s <= long_n:
-                h_step(s, w - s)
+        for depth in range(Q - 1):
+            events.append((s + depth if depth else 0, 0, s, "chain", depth))
+        events.append((s + Q - 2 + 0.1, 1, s, "inner", 0))
+        events.append((s + Q - 1, 1, s, "outer", 0))
+        for k in range(1, long_n + 1):
+            events.append((s + HOLD + k * PACE + 0.2, 2, s, "ring", k))
+    for _, _, s, kind, k in sorted(events):
+        if kind == "chain":
+            if k == 0:
+                sib[s].wait_recv()
+            with scope(f"chain#s={s}#k={k}"):
+                chain_step(s, k)
+        elif kind == "ring":
+            h_step(s, k)
+        else:
+            with scope(f"{kind}#s={s}"):
+
+                @pl.when(inner if kind == "inner" else jnp.logical_not(inner))
+                def _():
+                    finish(s)
 
     def block(bb):
         return acc[pl.ds(pl.multiple_of(bb * f, 8), f), :]
@@ -266,7 +285,8 @@
         o_sib_send[q] = block(q * CORES + 1 - core).astype(jnp.bfloat16)
     osib = remote(o_sib_send, o_sib_recv, os_ss, os_rs, sibling)
     osib.start()
-    osib.wait_recv()
+    with scope("osib"):
+        osib.wait_recv()
     outs = []
     for j in range(1, Q):
         q = lax.rem(p + j, Q)
@@ -276,9 +296,10 @@
         outs.append(c)
     total = block(b) + o_sib_recv[p].astype(jnp.float32)
     for j, c in enumerate(outs):
-        c.wait_recv()
+        with scope("oout"):
+            c.wait_recv()
         total = total + o_recv[j].astype(jnp.float32)
-    out_ref[...] = total.T.astype(jnp.bfloat16)
+    out_ref[...] = total.astype(jnp.bfloat16)
 
     for t in range(T):
         ring_drain(tok, tok_ss, tok_rs, t)
@@ -292,9 +313,9 @@
 
 
 def shards(G, tokens, gate_weight, up_weight, down_weight):
-    rows, f = tokens.shape
+    f, rows = tokens.shape
     _, depth, width = gate_weight.shape
-    _, down_depth, out_width = down_weight.shape
+    _, out_width, down_depth = down_weight.shape
     hb = width // XS
     R = hb // SSPLIT
     bf, f32 = jnp.bfloat16, jnp.float32
@@ -302,11 +323,12 @@
     V = pltpu.VMEM
     return pl.pallas_call(
         functools.partial(kernel, G),
-        out_shape=jax.ShapeDtypeStruct((rows, f), bf),
+        out_shape=jax.ShapeDtypeStruct((f, rows), bf),
         in_specs=[pl.BlockSpec(memory_space=pltpu.VMEM)] + [pl.BlockSpec(memory_space=pl.ANY)] * 3,
         out_specs=pl.BlockSpec(memory_space=pltpu.VMEM),
         scratch_shapes=[
             V((2, depth, width), bf),
+            V((out_width, down_depth), bf),
             V((down_depth, out_width), bf),
             V((2, width, depth), bf),
             V((TSPLIT, G, f, rows // TSPLIT), bf),
@@ -345,7 +367,15 @@
 
 def solution(mesh):
     G = mesh.shape["gx"] // XS
-    placed = (P("groups", "gx"), P("gx", None, None), P("gx", None, None), P("gx", None, None))
-    return jax.shard_map(
-        functools.partial(shards, G), mesh=mesh, in_specs=placed, out_specs=P("groups", "gx"), check_vma=False
+    body = jax.shard_map(
+        functools.partial(shards, G),
+        mesh=mesh,
+        in_specs=(P("gx", "groups"), P("gx", None, None), P("gx", None, None), P("gx", None, None)),
+        out_specs=P("gx", "groups"),
+        check_vma=False,
     )
+
+    def step(tokens, gate_weight, up_weight, down_weight):
+        return body(tokens.T, gate_weight, up_weight, jnp.swapaxes(down_weight, 1, 2)).T
+
+    return step

time: 194 us -> 177 us (0.912)
  the two profiles are of different devices: /device:TPU:37 before, /device:TPU:39 now
where the time goes in v2:
time: 177 us
  Pallas kernels  175 us (99%)
    pallas_call x1, Pallas kernels, shards(): pl.pallas_call(functools.partial(kernel, G), out_shape=jax.ShapeDtypeStru...  175 us

profile of v2, /device:TPU:39, one launch (start us, length us, event | category | flops | bytes accessed | tf_op | source)
XLA Modules:
  0.0 176.8 jit_solution(4339505049445236790)
XLA Ops:
  0.0 175.3 %shard_map.46 = bf16[72,384]{1,0:T(8,128)(2,1)} custom-call(bf16[72,384]{1,0:T(8,128)(2,1)} %bitcast.5, bf16[1,576,2304]{2,1,0:T(8,128)(2,1)} %gate_hbm.1, bf16[1,576,2304]{2,1,0:T(8,128)(2,1)} %up_hbm.1, bf16[1,576,2304]{2,1,0:T(8,128)(2,1)} %bitcast.3), custom_call_target="tpu_custom_call" | custom-call | tf_op jit(solution)/shard_map/pallas_call | solution.py:324
  175.3 1.4 copy.6

commit v3 on v2

--- a/solution.py
+++ b/solution.py
@@ -11,10 +11,7 @@
 XS = 8
 CORES = 2
 Q = XS // CORES
-TSPLIT = 3
-SSPLIT = 3
-HOLD = 5
-PACE = 1.5
+LANES = 128
 MESH = pl.DeviceIdType.MESH
 
 
@@ -65,11 +62,8 @@
     o_ss,
     o_rs,
 ):
-    S, T = SSPLIT, TSPLIT
-    f, tokens = tok_ref.shape
-    tl = tokens // T
-    R = hbuf.shape[2]
-    HB = R * S
+    f = tok_ref.shape[0]
+    T, HB, tl = hbuf.shape[0], hbuf.shape[2], hbuf.shape[3]
 
     me = lax.axis_index("gx")
     a = me // XS
@@ -92,9 +86,6 @@
         pltpu.make_async_copy(up_hbm.at[0], w_v.at[1], load_sem.at[1]),
         pltpu.make_async_copy(down_hbm.at[0], dt_v, load_sem.at[2]),
     ]
-    for c in loads:
-        c.start()
-
     for t in range(T):
         tok[t, a] = tok_ref[:, t * tl : (t + 1) * tl]
 
@@ -102,6 +93,8 @@
     peers = [long_to, short_to, sibling] + [chip(lax.rem(p + j, Q)) for j in range(1, Q)]
     for peer in peers:
         pl.semaphore_signal(barrier, inc=1, device_id=to(peer), device_id_type=MESH)
+    for c in loads:
+        c.start()
     with scope("barrier"):
         pl.semaphore_wait(barrier, len(peers))
 
@@ -137,9 +130,6 @@
         for k in range(1, short_n + 1):
             ring(buf, ss, rs, i, k, False).wait_send()
 
-    for t in range(T):
-        ring_start(tok, tok_ss, tok_rs, t)
-
     def turn(load, src, dst):
         load.wait()
         wide = 128
@@ -152,44 +142,32 @@
         lax.fori_loop(0, src.shape[1] // wide, body, 0)
 
     turns = [(loads[0], w_v.at[0], wt.at[0]), (loads[1], w_v.at[1], wt.at[1]), (loads[2], dt_v, d_v)]
-    for k in range(1, long_n + 1):
-        if k <= len(turns):
-            turn(*turns[k - 1])
-        for t in range(T):
-            with scope(f"tok#k={k}#t={t}"):
-                ring_step(tok, tok_ss, tok_rs, t, k)
-
-    for t in range(T):
+
+    def sums(t):
         for c in range(G):
-            x32[c * f : (c + 1) * f, t * tl : (t + 1) * tl] = tok[t, c].astype(jnp.float32)
-    xb[...] = x32[...].astype(jnp.bfloat16)
-
-    def part(q, g, of_core):
-        row = pl.multiple_of((q * CORES + of_core) * HB, 32)
-        return jnp.dot(wt[g, pl.ds(row, HB), :], xb[...], preferred_element_type=jnp.float32)
-
-    def sib_part(i, carry):
-        q, g = i // 2, lax.rem(i, 2)
-        r = part(q, g, 1 - core).astype(jnp.bfloat16)
-        for s in range(S):
-            sib_send[s, q, g] = r[s * R : (s + 1) * R]
-        return carry
-
-    with scope("sibpart"):
+            x32[c * f : (c + 1) * f, :] = tok[t, c].astype(jnp.float32)
+        xb[...] = x32[...].astype(jnp.bfloat16)
+
+        def part(q, g, of_core):
+            row = pl.multiple_of((q * CORES + of_core) * HB, 32)
+            return jnp.dot(wt[g, pl.ds(row, HB), :], xb[...], preferred_element_type=jnp.float32)
+
+        def sib_part(i, carry):
+            q, g = i // 2, lax.rem(i, 2)
+            sib_send[t, q, g] = part(q, g, 1 - core).astype(jnp.bfloat16)
+            return carry
+
+        def own_part(i, carry):
+            q, g = i // 2, lax.rem(i, 2)
+            own[t, q, g] = part(q, g, core)
+            return carry
+
         lax.fori_loop(0, Q * 2, sib_part, 0)
-    sib = [remote(sib_send.at[s], sib_recv.at[s], sib_ss.at[s], sib_rs.at[s], sibling) for s in range(S)]
-    for s in range(S):
-        sib[s].start()
-
-    def own_part(i, carry):
-        q, g = i // 2, lax.rem(i, 2)
-        r = part(q, g, core)
-        for s in range(S):
-            own[s, q, g] = r[s * R : (s + 1) * R]
-        return carry
-
-    with scope("ownpart"):
+        pair(t).start()
         lax.fori_loop(0, Q * 2, own_part, 0)
+
+    def pair(t):
+        return remote(sib_send.at[t], sib_recv.at[t], sib_ss.at[t], sib_rs.at[t], sibling)
 
     def chain(d, s, q):
         peer = chip(p + 1) if d == 0 else chip(p - 1)
@@ -242,9 +220,9 @@
     acc[...] = jnp.zeros_like(acc)
 
     def down(s, c):
-        row = pl.multiple_of(c * HB + s * R, 16)
-        acc[...] += lax.dot_general(
-            d_v[pl.ds(row, R), :], hbuf[s, c], (((0,), (0,)), ((), ())), preferred_element_type=jnp.float32
+        row = pl.multiple_of(c * HB, 32)
+        acc[s] += lax.dot_general(
+            d_v[pl.ds(row, HB), :], hbuf[s, c], (((0,), (0,)), ((), ())), preferred_element_type=jnp.float32
         )
 
     def h_step(s, k):
@@ -254,23 +232,78 @@
         if k <= short_n:
             down(s, group_at(k))
 
+    def block(s, bb):
+        return acc[s, pl.ds(pl.multiple_of(bb * f, 8), f), :]
+
+    def out_pair(s):
+        return remote(o_sib_send.at[s], o_sib_recv.at[s], os_ss.at[s], os_rs.at[s], sibling)
+
+    def out_to(s, j):
+        peer = chip(lax.rem(p + j, Q))
+        return remote(o_send.at[s, j - 1], o_recv.at[s, j - 1], o_ss.at[s, j - 1], o_rs.at[s, j - 1], peer)
+
+    def out_step(s, stage):
+        if stage == 0:
+            for q in range(Q):
+                o_sib_send[s, q] = block(s, q * CORES + 1 - core).astype(jnp.bfloat16)
+            out_pair(s).start()
+        elif stage == 1:
+            out_pair(s).wait_recv()
+            for j in range(1, Q):
+                q = lax.rem(p + j, Q)
+                v = block(s, q * CORES + core) + o_sib_recv[s, q].astype(jnp.float32)
+                o_send[s, j - 1] = v.astype(jnp.bfloat16)
+                out_to(s, j).start()
+        else:
+            total = block(s, b) + o_sib_recv[s, p].astype(jnp.float32)
+            for j in range(1, Q):
+                out_to(s, j).wait_recv()
+                total = total + o_recv[s, j - 1].astype(jnp.float32)
+            out_ref[:, s * tl : (s + 1) * tl] = total.astype(jnp.bfloat16)
+
     inner = jnp.logical_and(p > 0, p < Q - 1)
     events = []
-    for s in range(S):
-        for depth in range(Q - 1):
-            events.append((s + depth if depth else 0, 0, s, "chain", depth))
-        events.append((s + Q - 2 + 0.1, 1, s, "inner", 0))
-        events.append((s + Q - 1, 1, s, "outer", 0))
+    for s in range(T):
         for k in range(1, long_n + 1):
-            events.append((s + HOLD + k * PACE + 0.2, 2, s, "ring", k))
-    for _, _, s, kind, k in sorted(events):
-        if kind == "chain":
+            events.append((5.5 * k + 1.9 * s, s, "tokens", k))
+        start = 24.0 + 3.5 * s
+        events.append((start, s, "sums", 0))
+        events.append((start + 0.1, s, "chain", 0))
+        base = 25.0 + 10.0 * s
+        for depth in range(1, Q - 1):
+            events.append((base + 3.5 + 5.0 * depth, s, "chain", depth))
+        events.append((base + 17.0, s, "inner", 0))
+        events.append((base + 19.0, s, "outer", 0))
+        for k in range(1, long_n + 1):
+            events.append((base + 21.0 + 11.0 * k, s, "ring", k))
+        last = base + 21.0 + 11.0 * long_n
+        for stage, after in enumerate((0.1, 3.0, 10.0)):
+            events.append((last + after, s, "out", stage))
+
+    for t in range(T):
+        ring_start(tok, tok_ss, tok_rs, t)
+        if t < len(turns):
+            with scope(f"turn#t={t}"):
+                turn(*turns[t])
+    for t in range(T, len(turns)):
+        turn(*turns[t])
+    for _, s, kind, k in sorted(events):
+        if kind == "tokens":
+            with scope(f"tok#s={s}#k={k}"):
+                ring_step(tok, tok_ss, tok_rs, s, k)
+        elif kind == "sums":
+            with scope(f"sums#s={s}"):
+                sums(s)
+        elif kind == "chain":
             if k == 0:
-                sib[s].wait_recv()
+                pair(s).wait_recv()
             with scope(f"chain#s={s}#k={k}"):
                 chain_step(s, k)
         elif kind == "ring":
             h_step(s, k)
+        elif kind == "out":
+            with scope(f"out#s={s}#k={k}"):
+                out_step(s, k)
         else:
             with scope(f"{kind}#s={s}"):
 
@@ -278,38 +311,14 @@
                 def _():
                     finish(s)
 
-    def block(bb):
-        return acc[pl.ds(pl.multiple_of(bb * f, 8), f), :]
-
-    for q in range(Q):
-        o_sib_send[q] = block(q * CORES + 1 - core).astype(jnp.bfloat16)
-    osib = remote(o_sib_send, o_sib_recv, os_ss, os_rs, sibling)
-    osib.start()
-    with scope("osib"):
-        osib.wait_recv()
-    outs = []
-    for j in range(1, Q):
-        q = lax.rem(p + j, Q)
-        o_send[j - 1] = (block(q * CORES + core) + o_sib_recv[q].astype(jnp.float32)).astype(jnp.bfloat16)
-        c = remote(o_send.at[j - 1], o_recv.at[j - 1], o_ss.at[j - 1], o_rs.at[j - 1], chip(q))
-        c.start()
-        outs.append(c)
-    total = block(b) + o_sib_recv[p].astype(jnp.float32)
-    for j, c in enumerate(outs):
-        with scope("oout"):
-            c.wait_recv()
-        total = total + o_recv[j].astype(jnp.float32)
-    out_ref[...] = total.astype(jnp.bfloat16)
-
-    for t in range(T):
-        ring_drain(tok, tok_ss, tok_rs, t)
-    for s in range(S):
-        sib[s].wait_send()
+    for s in range(T):
+        ring_drain(tok, tok_ss, tok_rs, s)
+        pair(s).wait_send()
         chain_drain(s)
         ring_drain(hbuf, h_ss, h_rs, s)
-    osib.wait_send()
-    for c in outs:
-        c.wait_send()
+        out_pair(s).wait_send()
+        for j in range(1, Q):
+            out_to(s, j).wait_send()
 
 
 def shards(G, tokens, gate_weight, up_weight, down_weight):
@@ -317,7 +326,7 @@
     _, depth, width = gate_weight.shape
     _, out_width, down_depth = down_weight.shape
     hb = width // XS
-    R = hb // SSPLIT
+    T = rows // LANES
     bf, f32 = jnp.bfloat16, jnp.float32
     dma = pltpu.SemaphoreType.DMA
     V = pltpu.VMEM
@@ -331,33 +340,33 @@
             V((out_width, down_depth), bf),
             V((down_depth, out_width), bf),
             V((2, width, depth), bf),
-            V((TSPLIT, G, f, rows // TSPLIT), bf),
-            V((depth, rows), f32),
-            V((depth, rows), bf),
-            V((SSPLIT, Q, 2, R, rows), bf),
-            V((SSPLIT, Q, 2, R, rows), bf),
-            V((SSPLIT, Q, 2, R, rows), f32),
-            V((2, SSPLIT, Q, 2, R, rows), bf),
-            V((2, SSPLIT, Q, 2, R, rows), bf),
-            V((SSPLIT, G, R, rows), bf),
-            V((out_width, rows), f32),
-            V((Q, f, rows), bf),
-            V((Q, f, rows), bf),
-            V((Q - 1, f, rows), bf),
-            V((Q - 1, f, rows), bf),
+            V((T, G, f, LANES), bf),
+            V((depth, LANES), f32),
+            V((depth, LANES), bf),
+            V((T, Q, 2, hb, LANES), bf),
+            V((T, Q, 2, hb, LANES), bf),
+            V((T, Q, 2, hb, LANES), f32),
+            V((2, T, Q, 2, hb, LANES), bf),
+            V((2, T, Q, 2, hb, LANES), bf),
+            V((T, G, hb, LANES), bf),
+            V((T, out_width, LANES), f32),
+            V((T, Q, f, LANES), bf),
+            V((T, Q, f, LANES), bf),
+            V((T, Q - 1, f, LANES), bf),
+            V((T, Q - 1, f, LANES), bf),
             dma((3,)),
-            dma((TSPLIT, G - 1)),
-            dma((TSPLIT, G - 1)),
-            dma((SSPLIT,)),
-            dma((SSPLIT,)),
-            dma((2, SSPLIT, Q)),
-            dma((2, SSPLIT, Q)),
-            dma((SSPLIT, G - 1)),
-            dma((SSPLIT, G - 1)),
-            dma(()),
-            dma(()),
-            dma((Q - 1,)),
-            dma((Q - 1,)),
+            dma((T, G - 1)),
+            dma((T, G - 1)),
+            dma((T,)),
+            dma((T,)),
+            dma((2, T, Q)),
+            dma((2, T, Q)),
+            dma((T, G - 1)),
+            dma((T, G - 1)),
+            dma((T,)),
+            dma((T,)),
+            dma((T, Q - 1)),
+            dma((T, Q - 1)),
         ],
         compiler_params=pltpu.CompilerParams(
             collective_id=0, has_side_effects=True, vmem_limit_bytes=60 * 1024 * 1024

time: 177 us -> 172 us (0.972)
  the two profiles are of different devices: /device:TPU:39 before, /device:TPU:37 now
where the time goes in v3:
time: 172 us
  Pallas kernels  171 us (99%)
    pallas_call x1, Pallas kernels, shards(): pl.pallas_call(functools.partial(kernel, G), out_shape=jax.ShapeDtypeStru...  171 us

profile of v3, /device:TPU:37, one launch (start us, length us, event | category | flops | bytes accessed | tf_op | source)
XLA Modules:
  0.0 172.1 jit_solution(10268388134050808178)
XLA Ops:
  0.0 170.7 %shard_map.46 = bf16[72,384]{1,0:T(8,128)(2,1)} custom-call(bf16[72,384]{1,0:T(8,128)(2,1)} %bitcast.5, bf16[1,576,2304]{2,1,0:T(8,128)(2,1)} %gate_hbm.1, bf16[1,576,2304]{2,1,0:T(8,128)(2,1)} %up_hbm.1, bf16[1,576,2304]{2,1,0:T(8,128)(2,1)} %bitcast.3), custom_call_target="tpu_custom_call" | custom-call | tf_op jit(solution)/shard_map/pallas_call | solution.py:333
  170.7 1.4 copy.6

commit v4 on v3

--- a/solution.py
+++ b/solution.py
@@ -12,6 +12,7 @@
 CORES = 2
 Q = XS // CORES
 LANES = 128
+HALVES = 2
 MESH = pl.DeviceIdType.MESH
 
 
@@ -63,7 +64,10 @@
     o_rs,
 ):
     f = tok_ref.shape[0]
-    T, HB, tl = hbuf.shape[0], hbuf.shape[2], hbuf.shape[3]
+    T, HB, tl = own.shape[0], own.shape[3], own.shape[4]
+    HR = HB // HALVES
+    S = T * HALVES
+    rows_of = lambda s: slice((s % HALVES) * HR, (s % HALVES + 1) * HR)
 
     me = lax.axis_index("gx")
     a = me // XS
@@ -152,22 +156,38 @@
             row = pl.multiple_of((q * CORES + of_core) * HB, 32)
             return jnp.dot(wt[g, pl.ds(row, HB), :], xb[...], preferred_element_type=jnp.float32)
 
-        def sib_part(i, carry):
-            q, g = i // 2, lax.rem(i, 2)
-            sib_send[t, q, g] = part(q, g, 1 - core).astype(jnp.bfloat16)
+        def sib_part(j, carry):
+            q = first_q(j)
+            for g in range(2):
+                sib_send[t, q, g] = part(q, g, 1 - core).astype(jnp.bfloat16)
+            pair(t, q).start()
             return carry
 
-        def own_part(i, carry):
-            q, g = i // 2, lax.rem(i, 2)
-            own[t, q, g] = part(q, g, core)
-            return carry
-
-        lax.fori_loop(0, Q * 2, sib_part, 0)
-        pair(t).start()
-        lax.fori_loop(0, Q * 2, own_part, 0)
-
-    def pair(t):
-        return remote(sib_send.at[t], sib_recv.at[t], sib_ss.at[t], sib_rs.at[t], sibling)
+        lax.fori_loop(0, Q, sib_part, 0)
+        for j in range(Q):
+            q = first_q(j)
+            for g in range(2):
+                own[t, q, g] = part(q, g, core)
+            pair(t, q).wait_recv()
+            if j < Q - 1:
+                for s in range(t * HALVES, (t + 1) * HALVES):
+                    for d, qs in ((0, Q - 1 - j), (1, j)):
+
+                        @pl.when(is_first(d))
+                        def _():
+                            ch_send[d, s, qs] = chip_sum(s, qs).astype(jnp.bfloat16)
+                            chain(d, s, qs).start()
+
+    def first_q(j):
+        low = 1 - p // (Q // 2)
+        return low * (Q - 1 - j) + (1 - low) * j
+
+    def pair(t, q):
+        return remote(sib_send.at[t, q], sib_recv.at[t, q], sib_ss.at[t, q], sib_rs.at[t, q], sibling)
+
+    def chip_sum(s, q):
+        t = s // HALVES
+        return own[t, q, :, rows_of(s)] + sib_recv[t, q, :, rows_of(s)].astype(jnp.float32)
 
     def chain(d, s, q):
         peer = chip(p + 1) if d == 0 else chip(p - 1)
@@ -189,23 +209,23 @@
             @pl.when(p == (depth if d == 0 else Q - 1 - depth))
             def _():
                 for q in range(Q - 1, depth, -1) if d == 0 else range(Q - 1 - depth):
-                    v = own[s, q] + sib_recv[s, q].astype(jnp.float32)
-                    if depth > 0:
-                        chain_from(d, s, q).wait_recv()
-                        v = v + ch_recv[d, s, q].astype(jnp.float32)
+                    v = chip_sum(s, q)
+                    chain_from(d, s, q).wait_recv()
+                    v = v + ch_recv[d, s, q].astype(jnp.float32)
                     ch_send[d, s, q] = v.astype(jnp.bfloat16)
                     chain(d, s, q).start()
 
     def finish(s):
-        own[s, p] = own[s, p] + sib_recv[s, p].astype(jnp.float32)
+        t = s // HALVES
+        own[t, p, :, rows_of(s)] = chip_sum(s, p)
         for d in range(2):
 
             @pl.when(jnp.logical_not(is_first(d)))
             def _():
                 chain_from(d, s, p).wait_recv()
-                own[s, p] = own[s, p] + ch_recv[d, s, p].astype(jnp.float32)
-
-        hbuf[s, a] = (gelu(own[s, p, 0]) * own[s, p, 1]).astype(jnp.bfloat16)
+                own[t, p, :, rows_of(s)] = own[t, p, :, rows_of(s)] + ch_recv[d, s, p].astype(jnp.float32)
+
+        hbuf[s, a] = (gelu(own[t, p, 0, rows_of(s)]) * own[t, p, 1, rows_of(s)]).astype(jnp.bfloat16)
         ring_start(hbuf, h_ss, h_rs, s)
         down(s, a)
 
@@ -220,9 +240,9 @@
     acc[...] = jnp.zeros_like(acc)
 
     def down(s, c):
-        row = pl.multiple_of(c * HB, 32)
-        acc[s] += lax.dot_general(
-            d_v[pl.ds(row, HB), :], hbuf[s, c], (((0,), (0,)), ((), ())), preferred_element_type=jnp.float32
+        row = pl.multiple_of(c * HB + (s % HALVES) * HR, 16)
+        acc[s // HALVES] += lax.dot_general(
+            d_v[pl.ds(row, HR), :], hbuf[s, c], (((0,), (0,)), ((), ())), preferred_element_type=jnp.float32
         )
 
     def h_step(s, k):
@@ -263,22 +283,22 @@
 
     inner = jnp.logical_and(p > 0, p < Q - 1)
     events = []
-    for s in range(T):
+    for t in range(T):
         for k in range(1, long_n + 1):
-            events.append((5.5 * k + 1.9 * s, s, "tokens", k))
-        start = 24.0 + 3.5 * s
-        events.append((start, s, "sums", 0))
-        events.append((start + 0.1, s, "chain", 0))
-        base = 25.0 + 10.0 * s
+            events.append((5.7 * k + 1.9 * t, t, "tokens", k))
+        events.append((23.0 + 4.5 * t, t, "sums", 0))
+    for s in range(S):
+        base = 26.0 + 4.8 * s
         for depth in range(1, Q - 1):
-            events.append((base + 3.5 + 5.0 * depth, s, "chain", depth))
-        events.append((base + 17.0, s, "inner", 0))
-        events.append((base + 19.0, s, "outer", 0))
+            events.append((base + 2.5 + 3.5 * depth, s, "chain", depth))
+        events.append((base + 11.0, s, "inner", 0))
+        events.append((base + 13.5, s, "outer", 0))
         for k in range(1, long_n + 1):
-            events.append((base + 21.0 + 11.0 * k, s, "ring", k))
-        last = base + 21.0 + 11.0 * long_n
-        for stage, after in enumerate((0.1, 3.0, 10.0)):
-            events.append((last + after, s, "out", stage))
+            last = base + 9.0 + 13.5 * k
+            events.append((last, s, "ring", k))
+        if (s + 1) % HALVES == 0:
+            for stage, after in enumerate((0.1, 2.0, 10.0)):
+                events.append((last + after, s // HALVES, "out", stage))
 
     for t in range(T):
         ring_start(tok, tok_ss, tok_rs, t)
@@ -295,8 +315,6 @@
             with scope(f"sums#s={s}"):
                 sums(s)
         elif kind == "chain":
-            if k == 0:
-                pair(s).wait_recv()
             with scope(f"chain#s={s}#k={k}"):
                 chain_step(s, k)
         elif kind == "ring":
@@ -311,14 +329,16 @@
                 def _():
                     finish(s)
 
-    for s in range(T):
-        ring_drain(tok, tok_ss, tok_rs, s)
-        pair(s).wait_send()
+    for t in range(T):
+        ring_drain(tok, tok_ss, tok_rs, t)
+        for q in range(Q):
+            pair(t, q).wait_send()
+        out_pair(t).wait_send()
+        for j in range(1, Q):
+            out_to(t, j).wait_send()
+    for s in range(S):
         chain_drain(s)
         ring_drain(hbuf, h_ss, h_rs, s)
-        out_pair(s).wait_send()
-        for j in range(1, Q):
-            out_to(s, j).wait_send()
 
 
 def shards(G, tokens, gate_weight, up_weight, down_weight):
@@ -327,6 +347,7 @@
     _, out_width, down_depth = down_weight.shape
     hb = width // XS
     T = rows // LANES
+    S, hr = T * HALVES, hb // HALVES
     bf, f32 = jnp.bfloat16, jnp.float32
     dma = pltpu.SemaphoreType.DMA
     V = pltpu.VMEM
@@ -346,9 +367,9 @@
             V((T, Q, 2, hb, LANES), bf),
             V((T, Q, 2, hb, LANES), bf),
             V((T, Q, 2, hb, LANES), f32),
-            V((2, T, Q, 2, hb, LANES), bf),
-            V((2, T, Q, 2, hb, LANES), bf),
-            V((T, G, hb, LANES), bf),
+            V((2, S, Q, 2, hr, LANES), bf),
+            V((2, S, Q, 2, hr, LANES), bf),
+            V((S, G, hr, LANES), bf),
             V((T, out_width, LANES), f32),
             V((T, Q, f, LANES), bf),
             V((T, Q, f, LANES), bf),
@@ -357,12 +378,12 @@
             dma((3,)),
             dma((T, G - 1)),
             dma((T, G - 1)),
-            dma((T,)),
-            dma((T,)),
-            dma((2, T, Q)),
-            dma((2, T, Q)),
-            dma((T, G - 1)),
-            dma((T, G - 1)),
+            dma((T, Q)),
+            dma((T, Q)),
+            dma((2, S, Q)),
+            dma((2, S, Q)),
+            dma((S, G - 1)),
+            dma((S, G - 1)),
             dma((T,)),
             dma((T,)),
             dma((T, Q - 1)),

time: 172 us -> 164 us (0.953)
  Pallas kernels: 171 us -> 163 us
    pallas_call x1, Pallas kernels: 171 us -> 163 us  [shards(): pl.pallas_call(functools.partial(kernel, G), out_shape=jax.ShapeDtypeStru...]
where the time goes in v4:
time: 164 us
  Pallas kernels  163 us (99%)
    pallas_call x1, Pallas kernels, shards(): pl.pallas_call(functools.partial(kernel, G), out_shape=jax.ShapeDtypeStru...  163 us

profile of v4, /device:TPU:37, one launch (start us, length us, event | category | flops | bytes accessed | tf_op | source)
XLA Modules:
  0.0 164.0 jit_solution(4864719947930654825)
XLA Ops:
  0.0 162.6 %shard_map.46 = bf16[72,384]{1,0:T(8,128)(2,1)} custom-call(bf16[72,384]{1,0:T(8,128)(2,1)} %bitcast.5, bf16[1,576,2304]{2,1,0:T(8,128)(2,1)} %gate_hbm.1, bf16[1,576,2304]{2,1,0:T(8,128)(2,1)} %up_hbm.1, bf16[1,576,2304]{2,1,0:T(8,128)(2,1)} %bitcast.3), custom_call_target="tpu_custom_call" | custom-call | tf_op jit(solution)/shard_map/pallas_call | solution.py:354
  162.6 1.4 copy.6

commit v5 on v4

--- a/solution.py
+++ b/solution.py
@@ -44,6 +44,7 @@
     ch_send,
     ch_recv,
     hbuf,
+    h_in,
     acc,
     o_sib_send,
     o_sib_recv,
@@ -58,6 +59,8 @@
     ch_rs,
     h_ss,
     h_rs,
+    in_ss,
+    in_rs,
     os_ss,
     os_rs,
     o_ss,
@@ -85,6 +88,18 @@
     chip = lambda q: a * XS + q * CORES + core
     to = lambda index: {"gx": index}
 
+    upper = p // (Q // 2)
+    inner_p = 1 + upper * (Q - 3)
+    outer_p = upper * (Q - 1)
+    is_inner = jnp.logical_and(p > 0, p < Q - 1)
+    beyond = lax.rem(a + 2 * upper - 1 + G, G)
+    before = lax.rem(a - 2 * upper + 1 + G, G)
+    beyond_far = upper * (1 - core) + (1 - upper) * core
+    end_peer = beyond * XS + inner_p * CORES + core
+    inner_peer = before * XS + outer_p * CORES + core
+    inside = lax.rem((p + 1) // 2, 2)
+    cross = inside * inner_peer + (1 - inside) * end_peer
+
     loads = [
         pltpu.make_async_copy(gate_hbm.at[0], w_v.at[0], load_sem.at[0]),
         pltpu.make_async_copy(up_hbm.at[0], w_v.at[1], load_sem.at[1]),
@@ -94,7 +109,7 @@
         tok[t, a] = tok_ref[:, t * tl : (t + 1) * tl]
 
     barrier = pltpu.get_barrier_semaphore()
-    peers = [long_to, short_to, sibling] + [chip(lax.rem(p + j, Q)) for j in range(1, Q)]
+    peers = [long_to, short_to, sibling, cross] + [chip(lax.rem(p + j, Q)) for j in range(1, Q)]
     for peer in peers:
         pl.semaphore_signal(barrier, inc=1, device_id=to(peer), device_id_type=MESH)
     for c in loads:
@@ -169,18 +184,18 @@
             for g in range(2):
                 own[t, q, g] = part(q, g, core)
             pair(t, q).wait_recv()
-            if j < Q - 1:
+            if j < Q // 2:
                 for s in range(t * HALVES, (t + 1) * HALVES):
-                    for d, qs in ((0, Q - 1 - j), (1, j)):
-
-                        @pl.when(is_first(d))
+                    for d in range(2):
+
+                        @pl.when(p == d * (Q - 1))
                         def _():
-                            ch_send[d, s, qs] = chip_sum(s, qs).astype(jnp.bfloat16)
-                            chain(d, s, qs).start()
+                            chain_send(s, of_direction(d)[j], False)
 
     def first_q(j):
-        low = 1 - p // (Q // 2)
-        return low * (Q - 1 - j) + (1 - low) * j
+        h = j // (Q // 2)
+        low = (1 - h) * (Q // 2 + j) + h * (Q - 1 - j)
+        return (1 - upper) * low + upper * (Q - 1 - low)
 
     def pair(t, q):
         return remote(sib_send.at[t, q], sib_recv.at[t, q], sib_ss.at[t, q], sib_rs.at[t, q], sibling)
@@ -189,53 +204,91 @@
         t = s // HALVES
         return own[t, q, :, rows_of(s)] + sib_recv[t, q, :, rows_of(s)].astype(jnp.float32)
 
-    def chain(d, s, q):
-        peer = chip(p + 1) if d == 0 else chip(p - 1)
-        return remote(ch_send.at[d, s, q], ch_recv.at[d, s, q], ch_ss.at[d, s, q], ch_rs.at[d, s, q], peer)
-
-    def chain_from(d, s, q):
-        peer = chip(p - 1) if d == 0 else chip(p + 1)
-        return remote(ch_send.at[d, s, q], ch_recv.at[d, s, q], ch_ss.at[d, s, q], ch_rs.at[d, s, q], peer)
-
-    def is_first(d):
-        return p == 0 if d == 0 else p == Q - 1
-
-    def sends(d, q):
-        return p < q if d == 0 else p > q
+    def of_direction(d):
+        return list(range(Q // 2, Q)) if d == 0 else list(reversed(range(Q // 2)))
+
+    def chain(s, q, peer):
+        return remote(ch_send.at[s, q], ch_recv.at[s, q], ch_ss.at[s, q], ch_rs.at[s, q], peer)
+
+    def chain_to(s, q):
+        return chain(s, q, chip(p + 1) if q >= Q // 2 else chip(p - 1))
+
+    def chain_send(s, q, adds):
+        v = chip_sum(s, q)
+        if adds:
+            chain_to(s, q).wait_recv()
+            v = v + ch_recv[s, q].astype(jnp.float32)
+        ch_send[s, q] = v.astype(jnp.bfloat16)
+        chain_to(s, q).start()
 
     def chain_step(s, depth):
         for d in range(2):
 
             @pl.when(p == (depth if d == 0 else Q - 1 - depth))
             def _():
-                for q in range(Q - 1, depth, -1) if d == 0 else range(Q - 1 - depth):
-                    v = chip_sum(s, q)
-                    chain_from(d, s, q).wait_recv()
-                    v = v + ch_recv[d, s, q].astype(jnp.float32)
-                    ch_send[d, s, q] = v.astype(jnp.bfloat16)
-                    chain(d, s, q).start()
+                for q in of_direction(d):
+                    chain_send(s, q, True)
+
+    def to_inner(s):
+        return remote(h_in.at[s], hbuf.at[s, a], in_ss.at[s, 0], in_rs.at[s], chip(inner_p))
+
+    def to_beyond(s):
+        e = (1 - beyond_far) * long_n
+        return remote(h_in.at[s], hbuf.at[s, a], in_ss.at[s, 1], h_rs.at[s, e], end_peer)
 
     def finish(s):
         t = s // HALVES
-        own[t, p, :, rows_of(s)] = chip_sum(s, p)
-        for d in range(2):
-
-            @pl.when(jnp.logical_not(is_first(d)))
-            def _():
-                chain_from(d, s, p).wait_recv()
-                own[t, p, :, rows_of(s)] = own[t, p, :, rows_of(s)] + ch_recv[d, s, p].astype(jnp.float32)
-
-        hbuf[s, a] = (gelu(own[t, p, 0, rows_of(s)]) * own[t, p, 1, rows_of(s)]).astype(jnp.bfloat16)
+
+        def hidden(q):
+            own[t, q, :, rows_of(s)] = chip_sum(s, q)
+            chain(s, q, chip(inner_p)).wait_recv()
+            own[t, q, :, rows_of(s)] = own[t, q, :, rows_of(s)] + ch_recv[s, q].astype(jnp.float32)
+            return (gelu(own[t, q, 0, rows_of(s)]) * own[t, q, 1, rows_of(s)]).astype(jnp.bfloat16)
+
+        h_in[s] = hidden(inner_p)
+        to_inner(s).start()
+        to_beyond(s).start()
+        hbuf[s, a] = hidden(p)
         ring_start(hbuf, h_ss, h_rs, s)
         down(s, a)
 
+    def take(s):
+        to_inner(s).wait_recv()
+        inward(s, lambda copy: copy.start())
+        down(s, a)
+
+    def inward(s, act):
+        @pl.when(beyond_far == 0)
+        def _():
+            act(ring(hbuf, h_ss, h_rs, s, 1, True))
+
+        @pl.when(beyond_far == 1)
+        def _():
+            act(ring(hbuf, h_ss, h_rs, s, 1, False))
+
     def chain_drain(s):
-        for d in range(2):
-            for q in range(Q):
-
-                @pl.when(sends(d, q))
-                def _():
-                    chain(d, s, q).wait_send()
+        for q in range(Q):
+
+            @pl.when(p < Q - 1 if q >= Q // 2 else p > 0)
+            def _():
+                chain_to(s, q).wait_send()
+
+    def hidden_drain(s):
+        for k in range(2, long_n + 1):
+            ring(hbuf, h_ss, h_rs, s, k, True).wait_send()
+        for k in range(2, short_n + 1):
+            ring(hbuf, h_ss, h_rs, s, k, False).wait_send()
+
+        @pl.when(is_inner)
+        def _():
+            inward(s, lambda copy: copy.wait_send())
+
+        @pl.when(jnp.logical_not(is_inner))
+        def _():
+            ring(hbuf, h_ss, h_rs, s, 1, True).wait_send()
+            ring(hbuf, h_ss, h_rs, s, 1, False).wait_send()
+            to_inner(s).wait_send()
+            to_beyond(s).wait_send()
 
     acc[...] = jnp.zeros_like(acc)
 
@@ -281,21 +334,22 @@
                 total = total + o_recv[s, j - 1].astype(jnp.float32)
             out_ref[:, s * tl : (s + 1) * tl] = total.astype(jnp.bfloat16)
 
-    inner = jnp.logical_and(p > 0, p < Q - 1)
     events = []
     for t in range(T):
         for k in range(1, long_n + 1):
             events.append((5.7 * k + 1.9 * t, t, "tokens", k))
-        events.append((23.0 + 4.5 * t, t, "sums", 0))
+        events.append((23.0 + 3.2 * t, t, "sums", 0))
     for s in range(S):
-        base = 26.0 + 4.8 * s
+        base = 26.0 + 4.0 * s
         for depth in range(1, Q - 1):
-            events.append((base + 2.5 + 3.5 * depth, s, "chain", depth))
-        events.append((base + 11.0, s, "inner", 0))
-        events.append((base + 13.5, s, "outer", 0))
+            events.append((base + 1.0 + 4.0 * depth, s, "chain", depth))
+        events.append((base + 13.0, s, "finish", 0))
+        events.append((base + 15.9, s, "take", 0))
         for k in range(1, long_n + 1):
-            last = base + 9.0 + 13.5 * k
+            last = 53.0 + 5.5 * s + 13.5 * (k - 1)
             events.append((last, s, "ring", k))
+        if s < S - 1:
+            events.append((last + 3.0, s, "drain", 0))
         if (s + 1) % HALVES == 0:
             for stage, after in enumerate((0.1, 2.0, 10.0)):
                 events.append((last + after, s // HALVES, "out", stage))
@@ -322,23 +376,26 @@
         elif kind == "out":
             with scope(f"out#s={s}#k={k}"):
                 out_step(s, k)
+        elif kind == "drain":
+            chain_drain(s)
+            hidden_drain(s)
+            if s < T:
+                ring_drain(tok, tok_ss, tok_rs, s)
+                for q in range(Q):
+                    pair(s, q).wait_send()
+        elif kind == "finish":
+            with scope(f"finish#s={s}"):
+                pl.when(jnp.logical_not(is_inner))(functools.partial(finish, s))
         else:
-            with scope(f"{kind}#s={s}"):
-
-                @pl.when(inner if kind == "inner" else jnp.logical_not(inner))
-                def _():
-                    finish(s)
-
+            with scope(f"take#s={s}"):
+                pl.when(is_inner)(functools.partial(take, s))
+
+    chain_drain(S - 1)
+    hidden_drain(S - 1)
     for t in range(T):
-        ring_drain(tok, tok_ss, tok_rs, t)
-        for q in range(Q):
-            pair(t, q).wait_send()
         out_pair(t).wait_send()
         for j in range(1, Q):
             out_to(t, j).wait_send()
-    for s in range(S):
-        chain_drain(s)
-        ring_drain(hbuf, h_ss, h_rs, s)
 
 
 def shards(G, tokens, gate_weight, up_weight, down_weight):
@@ -367,9 +424,10 @@
             V((T, Q, 2, hb, LANES), bf),
             V((T, Q, 2, hb, LANES), bf),
             V((T, Q, 2, hb, LANES), f32),
-            V((2, S, Q, 2, hr, LANES), bf),
-            V((2, S, Q, 2, hr, LANES), bf),
+            V((S, Q, 2, hr, LANES), bf),
+            V((S, Q, 2, hr, LANES), bf),
             V((S, G, hr, LANES), bf),
+            V((S, hr, LANES), bf),
             V((T, out_width, LANES), f32),
             V((T, Q, f, LANES), bf),
             V((T, Q, f, LANES), bf),
@@ -380,10 +438,12 @@
             dma((T, G - 1)),
             dma((T, Q)),
             dma((T, Q)),
-            dma((2, S, Q)),
-            dma((2, S, Q)),
+            dma((S, Q)),
+            dma((S, Q)),
             dma((S, G - 1)),
             dma((S, G - 1)),
+            dma((S, 2)),
+            dma((S,)),
             dma((T,)),
             dma((T,)),
             dma((T, Q - 1)),

time: 164 us -> 172 us (1.049)
  Pallas kernels: 163 us -> 170 us
    pallas_call x1, Pallas kernels: 163 us -> 170 us  [shards(): pl.pallas_call(functools.partial(kernel, G), out_shape=jax.ShapeDtypeStru...]
where the time goes in v5:
time: 172 us
  Pallas kernels  170 us (99%)
    pallas_call x1, Pallas kernels, shards(): pl.pallas_call(functools.partial(kernel, G), out_shape=jax.ShapeDtypeStru...  170 us

profile of v5, /device:TPU:37, one launch (start us, length us, event | category | flops | bytes accessed | tf_op | source)
XLA Modules:
  0.0 171.5 jit_solution(11052648989177115818)
XLA Ops:
  0.0 170.1 %shard_map.46 = bf16[72,384]{1,0:T(8,128)(2,1)} custom-call(bf16[72,384]{1,0:T(8,128)(2,1)} %bitcast.5, bf16[1,576,2304]{2,1,0:T(8,128)(2,1)} %gate_hbm.1, bf16[1,576,2304]{2,1,0:T(8,128)(2,1)} %up_hbm.1, bf16[1,576,2304]{2,1,0:T(8,128)(2,1)} %bitcast.3), custom_call_target="tpu_custom_call" | custom-call | tf_op jit(solution)/shard_map/pallas_call | solution.py:411
  170.1 1.4 copy.6

commit v6 on v4

--- a/solution.py
+++ b/solution.py
@@ -296,6 +296,8 @@
         for k in range(1, long_n + 1):
             last = base + 9.0 + 13.5 * k
             events.append((last, s, "ring", k))
+        if s < S - 1:
+            events.append((last + 3.0, s, "drain", 0))
         if (s + 1) % HALVES == 0:
             for stage, after in enumerate((0.1, 2.0, 10.0)):
                 events.append((last + after, s // HALVES, "out", stage))
@@ -319,6 +321,13 @@
                 chain_step(s, k)
         elif kind == "ring":
             h_step(s, k)
+        elif kind == "drain":
+            chain_drain(s)
+            ring_drain(hbuf, h_ss, h_rs, s)
+            if s < T:
+                ring_drain(tok, tok_ss, tok_rs, s)
+                for q in range(Q):
+                    pair(s, q).wait_send()
         elif kind == "out":
             with scope(f"out#s={s}#k={k}"):
                 out_step(s, k)
@@ -329,16 +338,12 @@
                 def _():
                     finish(s)
 
+    chain_drain(S - 1)
+    ring_drain(hbuf, h_ss, h_rs, S - 1)
     for t in range(T):
-        ring_drain(tok, tok_ss, tok_rs, t)
-        for q in range(Q):
-            pair(t, q).wait_send()
         out_pair(t).wait_send()
         for j in range(1, Q):
             out_to(t, j).wait_send()
-    for s in range(S):
-        chain_drain(s)
-        ring_drain(hbuf, h_ss, h_rs, s)
 
 
 def shards(G, tokens, gate_weight, up_weight, down_weight):

time: 164 us -> 164 us (level)
  no operation moved by 1% of the time
where the time goes in v6:
time: 164 us
  Pallas kernels  163 us (99%)
    pallas_call x1, Pallas kernels, shards(): pl.pallas_call(functools.partial(kernel, G), out_shape=jax.ShapeDtypeStru...  163 us

profile of v6, /device:TPU:37, one launch (start us, length us, event | category | flops | bytes accessed | tf_op | source)
XLA Modules:
  0.0 164.0 jit_solution(8782859675933793634)
XLA Ops:
  0.0 162.5 %shard_map.46 = bf16[72,384]{1,0:T(8,128)(2,1)} custom-call(bf16[72,384]{1,0:T(8,128)(2,1)} %bitcast.5, bf16[1,576,2304]{2,1,0:T(8,128)(2,1)} %gate_hbm.1, bf16[1,576,2304]{2,1,0:T(8,128)(2,1)} %up_hbm.1, bf16[1,576,2304]{2,1,0:T(8,128)(2,1)} %bitcast.3), custom_call_target="tpu_custom_call" | custom-call | tf_op jit(solution)/shard_map/pallas_call | solution.py:359
  162.6 1.4 copy.6
